TPU v7x, 16 devices: a 4x2x1 block of a 4x4x8 slice. The times are simulated.
16 devices in a mesh: dp: 2 (over y, z), tp: 8 (over x, core).
Axes of the slice: x: 4, y: 2, z: 1, core: 2. Of those that a mesh axis runs over, the one named last changes fastest.
The devices are a block of a 4x4x8 slice.
Arguments:
- x_in: bfloat16 [512, 4096], P('dp'), parts along dimension 0
- w_q: bfloat16 [2, 4096, 4096], P(None, None, 'tp')
- w_k: bfloat16 [2, 4096, 1024], P(None, None, 'tp')
- w_v: bfloat16 [2, 4096, 1024], P(None, None, 'tp')
- w_o: bfloat16 [2, 4096, 4096], P(None, 'tp')
- w_gate: bfloat16 [2, 4096, 14336], P(None, None, 'tp')
- w_up: bfloat16 [2, 4096, 14336], P(None, None, 'tp')
- w_down: bfloat16 [2, 14336, 4096], P(None, 'tp')
- norm_gain: bfloat16 [2, 4096], replicated
- k_cache: bfloat16 [2, 512, 8, 64, 128], P(None, 'dp', 'tp'), parts along dimension 1
- v_cache: bfloat16 [2, 512, 8, 64, 128], P(None, 'dp', 'tp'), parts along dimension 1
- lengths: int32 [512], P('dp'), parts along dimension 0
Outputs:
- output 1: bfloat16 [512, 4096], P('dp'), parts along dimension 0
- output 2: bfloat16 [2, 512, 8, 128], P(None, 'dp', 'tp'), parts along dimension 1
- output 3: bfloat16 [2, 512, 8, 128], P(None, 'dp', 'tp'), parts along dimension 1
There are 2 independent parts. A program takes and returns all parts, laid end to end along the dimension named above; an argument that names none is the same for every part.
All inputs are finite; a program needn't handle non-finite values.
Results may differ from a plain program's by a relative error of at most 0.0169927.
Values are sent between devices in bfloat16 or wider.
A program may use at most 768 MiB of HBM per device.

v0:
```python
import functools
import math

import jax
import jax.numpy as jnp
import numpy as np
from jax import lax
from jax.experimental import pallas as pl
from jax.experimental.pallas import tpu as pltpu
from jax.sharding import PartitionSpec as P

ROPE_BASE = 10000
NORM_EPS = 1e-5
MESH = pl.DeviceIdType.MESH
F32 = jnp.float32
BF16 = jnp.bfloat16

ROW_GROUP = 8
KV_PIECES = 4
GROUPS = 4


def kernel(dims, x_hbm, wq, wk, wv, wo, wg, wu, wd, gain, kc, vc, lens, freq,
           xo, kn, vn,
           xb, acc, hb, wa, wb, kb, vb, lhs, qs, ks, vs, ob, lenb, cosb, sinb, rowscale, gains, kst, vst,
           send_d, recv_d, send_o, send_r, send_l, opp_t, opp_b, from_l, from_r, own, hold_r, hold_l, stat_s, stat_r,
           sem_a, sem_kv, sem_b, sem_x, sem_kn,
           d_send, d_recv, o_send, o_recv, r_send, l_send, fl_recv, fr_recv,
           ag_send, ag_fwd, ag_ring, ag_recv, st_send, st_recv):
    layers, rows, width, q_width, head, ff, cache_len, members = dims
    heads = q_width // head
    blk = width // members
    chunk = blk // 2
    half = rows // 2
    n_in = q_width + 2 * head + 2 * ff
    k_out = q_width + ff
    chips = members // 2

    me = lax.axis_index("tp")
    core = me % 2
    chip = me // 2
    mate = 2 * chip + 1 - core
    right_chip = (chip + 1) % chips
    left_chip = (chip + 3) % chips
    opp_chip = (chip + 2) % chips
    right = 2 * right_chip + core
    left = 2 * left_chip + core

    def dev(i):
        return {"tp": i}

    def chunk_id(g, q):
        turn = (g + (g // 2) * (2 * g - 3)) % 4
        if q % 2:
            turn = (4 - turn) % 4
        c = core if q < 2 else 1 - core
        return 2 * (2 * ((chip + turn) % chips) + c) + q % 2

    cols = ((wq, 0, q_width), (wk, q_width, head), (wv, q_width + head, head),
            (wg, q_width + 2 * head, ff), (wu, q_width + 2 * head + ff, ff))

    def a_copies(l, g, slot):
        out = []
        for q in range(4):
            row = pl.multiple_of(chunk_id(g, q) * chunk, chunk)
            for n, (w, at, size) in enumerate(cols):
                out.append(pltpu.make_async_copy(
                    w.at[l, pl.ds(row, chunk), :],
                    wa.at[slot, pl.ds(q * chunk, chunk), pl.ds(at, size)],
                    sem_a.at[slot, q, n]))
        return out

    piece = rows // KV_PIECES

    def kv_copies(l, p):
        at = pl.multiple_of(p * piece, piece)
        return [pltpu.make_async_copy(src.at[l, pl.ds(at, piece), 0], dst.at[pl.ds(at, piece)], sem_kv.at[n, p])
                for n, (src, dst) in enumerate(((kc, kb), (vc, vb)))]

    def b_copies(l):
        out = [pltpu.make_async_copy(wo.at[l], wb.at[pl.ds(0, q_width)], sem_b.at[0])]
        part = ff // 4
        for n in range(4):
            out.append(pltpu.make_async_copy(
                wd.at[l, pl.ds(n * part, part), :], wb.at[pl.ds(q_width + n * part, part)], sem_b.at[1 + n]))
        return out

    def x_copy(n):
        return pltpu.make_async_copy(x_hbm.at[:, pl.ds(n * chunk, chunk)], xb.at[n], sem_x.at[n])

    def out_copy(n):
        at = pl.multiple_of(n * chunk, chunk)
        return pltpu.make_async_copy(xb.at[n], xo.at[:, pl.ds(at, chunk)], sem_x.at[n])

    def kn_copies(l):
        return [pltpu.make_async_copy(kst, kn.at[l], sem_kn.at[0]), pltpu.make_async_copy(vst, vn.at[l], sem_kn.at[1])]

    def start(copies):
        for c in copies:
            c.start()

    def wait(copies):
        for c in copies:
            c.wait()

    def remote(src, dst, s, r, to):
        return pltpu.make_async_remote_copy(src_ref=src, dst_ref=dst, send_sem=s, recv_sem=r,
                                            device_id=dev(to), device_id_type=MESH)

    def mate_copy(n):
        return remote(send_d.at[n], recv_d.at[n], d_send.at[n], d_recv.at[n], mate)

    top, bottom = pl.ds(0, half), pl.ds(half, half)
    opp_right = remote(send_o.at[top], opp_t, o_send.at[0], o_recv.at[0], right)
    opp_left = remote(send_o.at[bottom], opp_b, o_send.at[1], o_recv.at[1], left)
    right_top = remote(send_r.at[top], from_l.at[top], r_send.at[0], fl_recv.at[0], right)
    right_bottom = remote(send_r.at[bottom], from_l.at[bottom], r_send.at[1], fl_recv.at[1], right)
    left_top = remote(send_l.at[top], from_r.at[top], l_send.at[0], fr_recv.at[0], left)
    left_bottom = remote(send_l.at[bottom], from_r.at[bottom], l_send.at[1], fr_recv.at[1], left)

    def x_send(n, s, to):
        return remote(xb.at[n], xb.at[n], s, ag_recv.at[n], to)

    own_a, own_b = 2 * me, 2 * me + 1
    own_sends = [x_send(own_a, ag_send.at[0], left), x_send(own_b, ag_send.at[1], right),
                 x_send(own_a, ag_send.at[2], mate), x_send(own_b, ag_send.at[3], mate),
                 x_send(own_b, ag_send.at[4], left), x_send(own_a, ag_send.at[5], right)]

    def mate_forward(g, q):
        return x_send(chunk_id(g, q), ag_fwd.at[g, q], mate)

    def ring_forward(q):
        return x_send(chunk_id(1, q), ag_ring.at[q], right if q else left)

    def arrived(n):
        x_send(n, ag_send.at[0], mate).wait_recv()

    def when(cond, fn):
        if isinstance(cond, bool):
            if cond:
                fn()
        else:
            pl.when(cond)(fn)

    def gather_step(g):
        def from_links():
            for q in range(2):
                arrived(chunk_id(g, q))
                when(g == 1, lambda q=q: ring_forward(q).start())
                mate_forward(g, q).start()
        when(g > 0, from_links)
        for q in range(2, 4):
            arrived(chunk_id(g, q))

    def gather_drain():
        for c in own_sends:
            c.wait_send()
        for g in range(1, GROUPS):
            for q in range(2):
                mate_forward(g, q).wait_send()
        for q in range(2):
            ring_forward(q).wait_send()

    def stat_copy(k):
        to = (me + k) % members
        return remote(stat_s, stat_r.at[k - 1], st_send.at[k - 1], st_recv.at[k - 1], to)

    for n in range(width // chunk):
        x_copy(n).start()
    start(a_copies(0, 0, 0))
    barrier = pltpu.get_barrier_semaphore()
    for k in range(1, members):
        pl.semaphore_signal(barrier, inc=1, device_id=dev((me + k) % members), device_id_type=MESH)
    start(a_copies(0, 1, 1))

    len_f = jnp.transpose(jnp.broadcast_to(lens[...].astype(F32), (head, rows)))
    lenb[...] = len_f
    angle = len_f * freq[...]
    cosb[...] = jnp.cos(angle)
    lane = lax.broadcasted_iota(jnp.int32, (rows, head), 1)
    sin = jnp.sin(angle)
    sinb[...] = jnp.where(lane < head // 2, -sin, sin)
    g32 = gain[...].astype(F32)
    for l in range(layers):
        gains[l] = g32[l:l + 1]

    total = jnp.zeros((rows, chunk), F32)
    for n in range(width // chunk):
        x_copy(n).wait()
    for n in range(width // chunk):
        v = xb[n].astype(F32)
        total = total + v * v
    mean = jnp.sum(total, axis=1, keepdims=True) / width
    rowscale[...] = jnp.broadcast_to(lax.rsqrt(mean + NORM_EPS), (rows, head))
    pl.semaphore_wait(barrier, members - 1)

    scale = 1.0 / math.sqrt(head)

    def layer(l, _):
        def norm_from_stats():
            s = stat_s[...]
            for k in range(1, members):
                stat_copy(k).wait_recv()
            for k in range(1, members):
                s = s + stat_r[k - 1]
            r = lax.rsqrt(s[0:1] / width + NORM_EPS)
            rowscale[...] = jnp.transpose(jnp.broadcast_to(r, (head, rows)))
        when(l > 0, norm_from_stats)

        def group(g, _):
            slot = g % 2
            when(l > 0, lambda: gather_step(g))
            r = rowscale[...]
            r = jnp.concatenate([r] * (chunk // head), axis=1)
            for q in range(4):
                n = chunk_id(g, q)
                gv = gains[l, :, pl.ds(pl.multiple_of(n * chunk, chunk), chunk)]
                hb[:, q * chunk:(q + 1) * chunk] = (xb[n].astype(F32) * r * gv).astype(BF16)
            wait(a_copies(l, g, slot))
            for at in range(0, n_in, 512):
                end = min(at + 512, n_in)
                d = jnp.dot(hb[...], wa[slot, :, at:end], preferred_element_type=F32)
                acc[:, at:end] = jnp.where(g == 0, d, acc[:, at:end] + d)
            when(g < GROUPS - 2, lambda: start(a_copies(l, g + 2, slot)))

            def later():
                for p in range(KV_PIECES):
                    start(kv_copies(l, p))
                start(b_copies(l))
            if layers > 1:
                pl.when(jnp.logical_and(l == 0, g == GROUPS - 2))(later)
            return 0
        lax.fori_loop(0, GROUPS, group, 0)

        cosv, sinv = cosb[...], sinb[...]
        for h in range(heads):
            v = acc[:, h * head:(h + 1) * head]
            qs[h] = (v * cosv + pltpu.roll(v, head // 2, 1) * sinv).astype(BF16).astype(F32)
        v = acc[:, q_width:q_width + head]
        kr = (v * cosv + pltpu.roll(v, head // 2, 1) * sinv).astype(BF16)
        vr = acc[:, q_width + head:q_width + 2 * head].astype(BF16)
        ks[...] = kr.astype(F32)
        vs[...] = vr.astype(F32)
        kst[...] = kr
        vst[...] = vr
        start(kn_copies(l))

        gate_at = q_width + 2 * head
        for at in range(0, ff, 256):
            gv = acc[:, gate_at + at:gate_at + at + 256]
            uv = acc[:, gate_at + ff + at:gate_at + ff + at + 256]
            lhs[:, q_width + at:q_width + at + 256] = (gv * jax.nn.sigmoid(gv) * uv).astype(BF16)

        tiles = ROW_GROUP * cache_len // head
        per_tile = head // cache_len
        r_id = lax.broadcasted_iota(jnp.int32, (1, ROW_GROUP, head), 1)
        lane3 = lax.broadcasted_iota(jnp.int32, (1, ROW_GROUP, head), 2)
        tile_of = r_id // per_tile
        in_row = (lane3 // cache_len) == (r_id % per_tile)
        slot_pos = (lane3 % cache_len).astype(F32)

        def attend(at):
            at = pl.multiple_of(at, ROW_GROUP)
            q3 = qs[:, pl.ds(at, ROW_GROUP), :]
            k_new = ks[pl.ds(at, ROW_GROUP), :][None]
            v_new = vs[pl.ds(at, ROW_GROUP), :][None]
            ln = lenb[pl.ds(at, ROW_GROUP), :][None]
            keys = kb[pl.ds(at, ROW_GROUP)].reshape(ROW_GROUP * cache_len, head)
            vals = vb[pl.ds(at, ROW_GROUP)].reshape(ROW_GROUP * cache_len, head)
            q2 = q3.reshape(heads * ROW_GROUP, head).astype(BF16)
            s = lax.dot_general(q2, keys, (((1,), (1,)), ((), ())), preferred_element_type=F32)
            pick = s[:, 0:head].reshape(heads, ROW_GROUP, head)
            for j in range(1, tiles):
                pick = jnp.where(tile_of == j, s[:, j * head:(j + 1) * head].reshape(heads, ROW_GROUP, head), pick)
            ok = jnp.logical_and(in_row, slot_pos < ln)
            sc = jnp.where(ok, pick * scale, -jnp.inf)
            s_new = jnp.sum(q3 * k_new, axis=-1, keepdims=True) * scale
            peak = jnp.maximum(jnp.max(sc, axis=-1, keepdims=True), s_new)
            w = jnp.exp(sc - peak)
            w_new = jnp.exp(s_new - peak)
            den = jnp.sum(w, axis=-1, keepdims=True) + w_new
            parts = [jnp.where(tile_of == j, w, 0.0).reshape(heads * ROW_GROUP, head).astype(BF16) for j in range(tiles)]
            pv = jnp.dot(jnp.concatenate(parts, axis=1), vals, preferred_element_type=F32)
            o = (pv.reshape(heads, ROW_GROUP, head) + w_new.astype(BF16).astype(F32) * v_new) / den
            for h in range(heads):
                ob[pl.ds(at, ROW_GROUP), h * head:(h + 1) * head] = o[h]

        def attend_piece(p, _):
            wait(kv_copies(l, p))

            def step(i, _):
                for u in range(2):
                    attend(p * piece + i * (2 * ROW_GROUP) + u * ROW_GROUP)
                return 0
            lax.fori_loop(0, piece // (2 * ROW_GROUP), step, 0)
            return 0
        lax.fori_loop(0, KV_PIECES, attend_piece, 0)
        lhs[:, 0:q_width] = ob[...].astype(BF16)

        def prefetch():
            start(a_copies(l + 1, 0, 0))
            for p in range(KV_PIECES):
                start(kv_copies(l + 1, p))
            start(a_copies(l + 1, 1, 1))
        when(l < layers - 1, prefetch)
        wait(kn_copies(l))
        when(l > 0, gather_drain)

        wait(b_copies(l))

        def share(i):
            at = pl.multiple_of(i * blk, blk)
            return jnp.dot(lhs[...], wb[:, pl.ds(at, blk)], preferred_element_type=F32)

        send_d[0] = share(2 * opp_chip + 1 - core).astype(BF16)
        mate_copy(0).start()
        send_d[1] = share(2 * right_chip + 1 - core).astype(BF16)
        mate_copy(1).start()
        t = share(2 * opp_chip + core)
        mate_copy(0).wait_recv()
        send_o[...] = (t + recv_d[0].astype(F32)).astype(BF16)
        opp_right.start()
        opp_left.start()
        send_d[2] = share(2 * left_chip + 1 - core).astype(BF16)
        mate_copy(2).start()
        t = share(right)
        mate_copy(1).wait_recv()
        t = t + recv_d[1].astype(F32)
        send_r[bottom] = t[half:].astype(BF16)
        right_bottom.start()
        hold_r[...] = t[:half]
        t = share(left)
        mate_copy(2).wait_recv()
        t = t + recv_d[2].astype(F32)
        send_l[top] = t[:half].astype(BF16)
        left_top.start()
        hold_l[...] = t[half:]
        send_d[3] = share(mate).astype(BF16)
        mate_copy(3).start()
        own[...] = share(me)
        when(l < layers - 1, lambda: start(b_copies(l + 1)))
        opp_right.wait_recv()
        send_r[top] = (hold_r[...] + opp_t[...].astype(F32)).astype(BF16)
        right_top.start()
        opp_left.wait_recv()
        send_l[bottom] = (hold_l[...] + opp_b[...].astype(F32)).astype(BF16)
        left_bottom.start()
        mate_copy(3).wait_recv()
        x_old = jnp.concatenate([xb[own_a], xb[own_b]], axis=1).astype(F32)
        own[...] = own[...] + recv_d[3].astype(F32) + x_old
        right_bottom.wait_recv()
        left_top.wait_recv()
        right_top.wait_recv()
        left_bottom.wait_recv()
        x_new = (own[...] + from_l[...].astype(F32) + from_r[...].astype(F32)).astype(BF16)
        xb[own_a] = x_new[:, :chunk]
        xb[own_b] = x_new[:, chunk:]

        def send_stats():
            v = x_new.astype(F32)
            v = v * v
            part = v[:, 0:head]
            for at in range(head, blk, head):
                part = part + v[:, at:at + head]
            col = jnp.broadcast_to(jnp.sum(part, axis=1, keepdims=True), (rows, head))
            stat_s[...] = jnp.transpose(col)[0:8]
            for k in range(1, members):
                stat_copy(k).start()
        when(l < layers - 1, send_stats)
        for c in own_sends:
            c.start()
        for n in range(4):
            mate_copy(n).wait_send()
        for c in (opp_right, opp_left, right_top, right_bottom, left_top, left_bottom):
            c.wait_send()

        def drain_stats():
            for k in range(1, members):
                stat_copy(k).wait_send()
        when(l < layers - 1, drain_stats)
        return 0

    lax.fori_loop(0, layers, layer, 0)

    out_copy(own_a).start()
    out_copy(own_b).start()
    for g in range(1, GROUPS):
        for q in range(2):
            arrived(chunk_id(g, q))
            if g == 1:
                ring_forward(q).start()
            mate_forward(g, q).start()
            out_copy(chunk_id(g, q)).start()
    for g in range(GROUPS):
        for q in range(2, 4):
            arrived(chunk_id(g, q))
            out_copy(chunk_id(g, q)).start()
    gather_drain()
    for n in range(width // chunk):
        out_copy(n).wait()


def solution(mesh):
    members = mesh.shape["tp"]
    weight_col = P(None, None, "tp")
    weight_row = P(None, "tp", None)
    cache_spec = P(None, "dp", "tp", None, None)
    new_spec = P(None, "dp", "tp", None)
    row_spec = P("dp", None)
    arg_specs = (row_spec, weight_col, weight_col, weight_col, weight_row, weight_col, weight_col, weight_row,
                 P(None, None), cache_spec, cache_spec, P("dp"))

    def per_device(x_in, w_q, w_k, w_v, w_o, w_gate, w_up, w_down, norm_gain, k_cache, v_cache, lengths):
        rows, width = x_in.shape
        layers, _, q_width = w_q.shape
        cache_len, head = k_cache.shape[-2:]
        ff = w_gate.shape[-1]
        dims = (layers, rows, width, q_width, head, ff, cache_len, members)
        blk = width // members
        chunk = blk // 2
        half = rows // 2
        n_in = q_width + 2 * head + 2 * ff
        inv = np.float32(ROPE_BASE) ** (-np.arange(head // 2, dtype=np.float32) / np.float32(head // 2))
        freq = jnp.asarray(np.concatenate([inv, inv])[None].astype(np.float32))
        vmem = pl.BlockSpec(memory_space=pltpu.VMEM)
        hbm = pl.BlockSpec(memory_space=pl.ANY)
        dma = pltpu.SemaphoreType.DMA
        x_out, k_new, v_new = pl.pallas_call(
            functools.partial(kernel, dims),
            out_shape=(jax.ShapeDtypeStruct((rows, width), BF16),
                       jax.ShapeDtypeStruct((layers, rows, head), BF16),
                       jax.ShapeDtypeStruct((layers, rows, head), BF16)),
            in_specs=[hbm] * 8 + [vmem, hbm, hbm, vmem, vmem],
            out_specs=(hbm, hbm, hbm),
            scratch_shapes=[
                pltpu.VMEM((width // chunk, rows, chunk), BF16),
                pltpu.VMEM((rows, n_in), F32),
                pltpu.VMEM((rows, 4 * chunk), BF16),
                pltpu.VMEM((2, 4 * chunk, n_in), BF16),
                pltpu.VMEM((q_width + ff, width), BF16),
                pltpu.VMEM((rows, cache_len, head), BF16),
                pltpu.VMEM((rows, cache_len, head), BF16),
                pltpu.VMEM((rows, q_width + ff), BF16),
                pltpu.VMEM((q_width // head, rows, head), F32),
                pltpu.VMEM((rows, head), F32),
                pltpu.VMEM((rows, head), F32),
                pltpu.VMEM((rows, q_width), F32),
                pltpu.VMEM((rows, head), F32),
                pltpu.VMEM((rows, head), F32),
                pltpu.VMEM((rows, head), F32),
                pltpu.VMEM((rows, head), F32),
                pltpu.VMEM((layers, 1, width), F32),
                pltpu.VMEM((rows, head), BF16),
                pltpu.VMEM((rows, head), BF16),
                pltpu.VMEM((4, rows, blk), BF16),
                pltpu.VMEM((4, rows, blk), BF16),
                pltpu.VMEM((rows, blk), BF16),
                pltpu.VMEM((rows, blk), BF16),
                pltpu.VMEM((rows, blk), BF16),
                pltpu.VMEM((half, blk), BF16),
                pltpu.VMEM((half, blk), BF16),
                pltpu.VMEM((rows, blk), BF16),
                pltpu.VMEM((rows, blk), BF16),
                pltpu.VMEM((rows, blk), F32),
                pltpu.VMEM((half, blk), F32),
                pltpu.VMEM((half, blk), F32),
                pltpu.VMEM((8, rows), F32),
                pltpu.VMEM((members - 1, 8, rows), F32),
                dma((2, 4, 5)), dma((2, KV_PIECES)), dma((5,)), dma((width // chunk,)), dma((2,)),
                dma((4,)), dma((4,)), dma((2,)), dma((2,)), dma((2,)), dma((2,)), dma((2,)), dma((2,)),
                dma((6,)), dma((GROUPS, 2)), dma((2,)), dma((width // chunk,)),
                dma((members - 1,)), dma((members - 1,)),
            ],
            compiler_params=pltpu.CompilerParams(
                collective_id=0, has_side_effects=True, vmem_limit_bytes=67043328),
        )(x_in, w_q, w_k, w_v, w_o, w_gate, w_up, w_down, norm_gain, k_cache, v_cache,
          lengths.reshape(1, rows), freq)
        return x_out, k_new.reshape(layers, rows, 1, head), v_new.reshape(layers, rows, 1, head)

    return jax.shard_map(per_device, mesh=mesh, in_specs=arg_specs, out_specs=(row_spec, new_spec, new_spec),
                         check_vma=False)
```

profile of v0, /device:TPU:113, one launch (start us, length us, event | category | flops | bytes accessed | tf_op | source)
XLA Modules:
  0.0 107.9 jit_solution(5055721691015068583)
XLA Ops:
  0.6 101.0 %shard_map.148 = (bf16[256,4096]{1,0:T(8,128)(2,1)}, bf16[2,256,128]{2,1,0:T(8,128)(2,1)}, bf16[2,256,128]{2,1,0:T(8,128)(2,1)}) custom-call(bf16[256,4096]{1,0:T(8,128)(2,1)} %x_hbm.1, bf16[2,4096,512]{2,1,0:T(8,128)(2,1)} %wq.1, bf16[2,4096,128]{2,1,0:T(8,128)(2,1)} %wk.1, bf16[2,4096,128]{2,1,0:T(8,128)(2,1)} %wv.1, bf16[2,512,4096]{2,1,0:T(8,128)(2,1)} %wo.1, ...), custom_call_target="tpu_custom_call" | custom-call | tf_op jit(solution)/shard_map/pallas_call | solution.py:428
  101.6 3.1 %copy.21 = bf16[256,4096]{1,0:T(8,128)(2,1)} copy(bf16[256,4096]{1,0:T(8,128)(2,1)} %get-tuple-element.15) | data formatting | bytes 4194304
  104.7 1.6 %copy.22 = bf16[2,256,1,128]{3,1,2,0:T(8,128)(2,1)} copy(bf16[2,256,1,128]{3,1,2,0:T(8,128)(2,1)} %bitcast.8) | data formatting | bytes 262144
  106.3 1.6 %copy.23 = bf16[2,256,1,128]{3,1,2,0:T(8,128)(2,1)} copy(bf16[2,256,1,128]{3,1,2,0:T(8,128)(2,1)} %bitcast.7) | data formatting | bytes 262144
where the time goes:
time: 108 us
  Pallas kernels  101 us (94%)
  local copies, waits for them, and re-layouts  6.26 us (6%)
    pallas_call x1, Pallas kernels, per_device(): pl.pallas_call(functools.partial(kernel, dims), out_shape=(jax.ShapeDtype...  101 us
    unnamed x3, local copies, waits for them, and re-layouts  6.26 us

commit v1 on v0

--- a/solution.py
+++ b/solution.py
@@ -16,7 +16,9 @@
 BF16 = jnp.bfloat16
 
 ROW_GROUP = 8
+STEP_ROWS = 32
 KV_PIECES = 4
+PLACE_PIECES = 8
 GROUPS = 4
 
 
@@ -59,11 +61,12 @@
     cols = ((wq, 0, q_width), (wk, q_width, head), (wv, q_width + head, head),
             (wg, q_width + 2 * head, ff), (wu, q_width + 2 * head + ff, ff))
 
-    def a_copies(l, g, slot):
+    def a_copies(l, g, slot, which=range(5)):
         out = []
         for q in range(4):
             row = pl.multiple_of(chunk_id(g, q) * chunk, chunk)
-            for n, (w, at, size) in enumerate(cols):
+            for n in which:
+                w, at, size = cols[n]
                 out.append(pltpu.make_async_copy(
                     w.at[l, pl.ds(row, chunk), :],
                     wa.at[slot, pl.ds(q * chunk, chunk), pl.ds(at, size)],
@@ -71,6 +74,10 @@
         return out
 
     piece = rows // KV_PIECES
+
+    def start_kv(l):
+        for p in range(KV_PIECES):
+            start(kv_copies(l, p))
 
     def kv_copies(l, p):
         at = pl.multiple_of(p * piece, piece)
@@ -142,15 +149,21 @@
         else:
             pl.when(cond)(fn)
 
-    def gather_step(g):
-        def from_links():
-            for q in range(2):
-                arrived(chunk_id(g, q))
-                when(g == 1, lambda q=q: ring_forward(q).start())
-                mate_forward(g, q).start()
-        when(g > 0, from_links)
+    def gather_links(g):
+        for q in range(2):
+            arrived(chunk_id(g, q))
+            when(g == 1, lambda q=q: ring_forward(q).start())
+            mate_forward(g, q).start()
+
+    def gather_mate(g):
         for q in range(2, 4):
             arrived(chunk_id(g, q))
+
+    def sum_drain():
+        for n in range(4):
+            mate_copy(n).wait_send()
+        for c in (opp_right, opp_left, right_top, right_bottom, left_top, left_bottom):
+            c.wait_send()
 
     def gather_drain():
         for c in own_sends:
@@ -187,7 +200,6 @@
     total = jnp.zeros((rows, chunk), F32)
     for n in range(width // chunk):
         x_copy(n).wait()
-    for n in range(width // chunk):
         v = xb[n].astype(F32)
         total = total + v * v
     mean = jnp.sum(total, axis=1, keepdims=True) / width
@@ -209,7 +221,7 @@
 
         def group(g, _):
             slot = g % 2
-            when(l > 0, lambda: gather_step(g))
+            when(l > 0, lambda: gather_mate(g))
             r = rowscale[...]
             r = jnp.concatenate([r] * (chunk // head), axis=1)
             for q in range(4):
@@ -217,18 +229,23 @@
                 gv = gains[l, :, pl.ds(pl.multiple_of(n * chunk, chunk), chunk)]
                 hb[:, q * chunk:(q + 1) * chunk] = (xb[n].astype(F32) * r * gv).astype(BF16)
             wait(a_copies(l, g, slot))
-            for at in range(0, n_in, 512):
-                end = min(at + 512, n_in)
+
+            def product(at, end):
                 d = jnp.dot(hb[...], wa[slot, :, at:end], preferred_element_type=F32)
                 acc[:, at:end] = jnp.where(g == 0, d, acc[:, at:end] + d)
-            when(g < GROUPS - 2, lambda: start(a_copies(l, g + 2, slot)))
-
-            def later():
-                for p in range(KV_PIECES):
-                    start(kv_copies(l, p))
-                start(b_copies(l))
-            if layers > 1:
-                pl.when(jnp.logical_and(l == 0, g == GROUPS - 2))(later)
+
+            cuts = list(range(0, n_in, 512)) + [n_in]
+            gate_end = q_width + 2 * head + ff
+            middle = next(n for n, at in enumerate(cuts) if at >= gate_end)
+            for at, end in zip(cuts[:middle], cuts[1:middle + 1]):
+                product(at, end)
+            when(g < GROUPS - 2, lambda: start(a_copies(l, g + 2, slot, range(4))))
+            pl.when(jnp.logical_and(l > 0, g < GROUPS - 1))(lambda: gather_links(g + 1))
+            pl.when(jnp.logical_and(l == 0, g == GROUPS - 2))(lambda: start_kv(l))
+            for at, end in zip(cuts[middle:-1], cuts[middle + 1:]):
+                product(at, end)
+            when(g < GROUPS - 2, lambda: start(a_copies(l, g + 2, slot, range(4, 5))))
+            pl.when(jnp.logical_and(l == 0, g == GROUPS - 2))(lambda: start(b_copies(l)))
             return 0
         lax.fori_loop(0, GROUPS, group, 0)
 
@@ -259,52 +276,62 @@
         in_row = (lane3 // cache_len) == (r_id % per_tile)
         slot_pos = (lane3 % cache_len).astype(F32)
 
-        def attend(at):
-            at = pl.multiple_of(at, ROW_GROUP)
-            q3 = qs[:, pl.ds(at, ROW_GROUP), :]
-            k_new = ks[pl.ds(at, ROW_GROUP), :][None]
-            v_new = vs[pl.ds(at, ROW_GROUP), :][None]
-            ln = lenb[pl.ds(at, ROW_GROUP), :][None]
-            keys = kb[pl.ds(at, ROW_GROUP)].reshape(ROW_GROUP * cache_len, head)
-            vals = vb[pl.ds(at, ROW_GROUP)].reshape(ROW_GROUP * cache_len, head)
-            q2 = q3.reshape(heads * ROW_GROUP, head).astype(BF16)
+        def scores(at):
+            keys = kb[at:at + ROW_GROUP].reshape(ROW_GROUP * cache_len, head)
+            q2 = qs[:, at:at + ROW_GROUP, :].reshape(heads * ROW_GROUP, head).astype(BF16)
             s = lax.dot_general(q2, keys, (((1,), (1,)), ((), ())), preferred_element_type=F32)
             pick = s[:, 0:head].reshape(heads, ROW_GROUP, head)
             for j in range(1, tiles):
                 pick = jnp.where(tile_of == j, s[:, j * head:(j + 1) * head].reshape(heads, ROW_GROUP, head), pick)
-            ok = jnp.logical_and(in_row, slot_pos < ln)
+            return pick
+
+        def weights(at, pick):
+            ok = jnp.logical_and(in_row, slot_pos < lenb[at:at + ROW_GROUP, :][None])
             sc = jnp.where(ok, pick * scale, -jnp.inf)
-            s_new = jnp.sum(q3 * k_new, axis=-1, keepdims=True) * scale
+            s_new = jnp.sum(qs[:, at:at + ROW_GROUP, :] * ks[at:at + ROW_GROUP, :][None], axis=-1, keepdims=True) * scale
             peak = jnp.maximum(jnp.max(sc, axis=-1, keepdims=True), s_new)
             w = jnp.exp(sc - peak)
             w_new = jnp.exp(s_new - peak)
-            den = jnp.sum(w, axis=-1, keepdims=True) + w_new
+            return w, w_new, jnp.sum(w, axis=-1, keepdims=True) + w_new
+
+        def mix(at, w, w_new, den):
+            vals = vb[at:at + ROW_GROUP].reshape(ROW_GROUP * cache_len, head)
             parts = [jnp.where(tile_of == j, w, 0.0).reshape(heads * ROW_GROUP, head).astype(BF16) for j in range(tiles)]
             pv = jnp.dot(jnp.concatenate(parts, axis=1), vals, preferred_element_type=F32)
-            o = (pv.reshape(heads, ROW_GROUP, head) + w_new.astype(BF16).astype(F32) * v_new) / den
+            o = (pv.reshape(heads, ROW_GROUP, head) + w_new.astype(BF16).astype(F32) * vs[at:at + ROW_GROUP, :][None]) / den
             for h in range(heads):
-                ob[pl.ds(at, ROW_GROUP), h * head:(h + 1) * head] = o[h]
-
-        def attend_piece(p, _):
+                ob[at:at + ROW_GROUP, h * head:(h + 1) * head] = o[h]
+
+        for p in range(KV_PIECES):
             wait(kv_copies(l, p))
-
-            def step(i, _):
-                for u in range(2):
-                    attend(p * piece + i * (2 * ROW_GROUP) + u * ROW_GROUP)
-                return 0
-            lax.fori_loop(0, piece // (2 * ROW_GROUP), step, 0)
-            return 0
-        lax.fori_loop(0, KV_PIECES, attend_piece, 0)
+        step = STEP_ROWS
+        groups_at = [list(range(b, b + step, ROW_GROUP)) for b in range(0, rows, step)]
+        picks, wts = {}, {}
+        for b in range(len(groups_at) + 2):
+            if b < len(groups_at):
+                for at in groups_at[b]:
+                    picks[at] = scores(at)
+            if 0 <= b - 2:
+                for at in groups_at[b - 2]:
+                    mix(at, *wts.pop(at))
+            if 0 <= b - 1 < len(groups_at):
+                for at in groups_at[b - 1]:
+                    wts[at] = weights(at, picks.pop(at))
         lhs[:, 0:q_width] = ob[...].astype(BF16)
 
         def prefetch():
             start(a_copies(l + 1, 0, 0))
-            for p in range(KV_PIECES):
-                start(kv_copies(l + 1, p))
+            start_kv(l + 1)
             start(a_copies(l + 1, 1, 1))
         when(l < layers - 1, prefetch)
         wait(kn_copies(l))
-        when(l > 0, gather_drain)
+
+        def drain():
+            sum_drain()
+            gather_drain()
+            for k in range(1, members):
+                stat_copy(k).wait_send()
+        when(l > 0, drain)
 
         wait(b_copies(l))
 
@@ -314,11 +341,11 @@
 
         send_d[0] = share(2 * opp_chip + 1 - core).astype(BF16)
         mate_copy(0).start()
+        own[...] = share(2 * opp_chip + core)
         send_d[1] = share(2 * right_chip + 1 - core).astype(BF16)
         mate_copy(1).start()
-        t = share(2 * opp_chip + core)
         mate_copy(0).wait_recv()
-        send_o[...] = (t + recv_d[0].astype(F32)).astype(BF16)
+        send_o[...] = (own[...] + recv_d[0].astype(F32)).astype(BF16)
         opp_right.start()
         opp_left.start()
         send_d[2] = share(2 * left_chip + 1 - core).astype(BF16)
@@ -369,15 +396,6 @@
         when(l < layers - 1, send_stats)
         for c in own_sends:
             c.start()
-        for n in range(4):
-            mate_copy(n).wait_send()
-        for c in (opp_right, opp_left, right_top, right_bottom, left_top, left_bottom):
-            c.wait_send()
-
-        def drain_stats():
-            for k in range(1, members):
-                stat_copy(k).wait_send()
-        when(l < layers - 1, drain_stats)
         return 0
 
     lax.fori_loop(0, layers, layer, 0)
@@ -385,19 +403,36 @@
     out_copy(own_a).start()
     out_copy(own_b).start()
     for g in range(1, GROUPS):
+        gather_links(g)
         for q in range(2):
-            arrived(chunk_id(g, q))
-            if g == 1:
-                ring_forward(q).start()
-            mate_forward(g, q).start()
             out_copy(chunk_id(g, q)).start()
     for g in range(GROUPS):
+        gather_mate(g)
         for q in range(2, 4):
-            arrived(chunk_id(g, q))
             out_copy(chunk_id(g, q)).start()
+    sum_drain()
     gather_drain()
     for n in range(width // chunk):
         out_copy(n).wait()
+
+
+def place(x, kn, vn, xo, ko, vo, xt, kt, vt, sem_in, sem_out):
+    part = x.shape[0] // PLACE_PIECES
+    loads, stores = [], []
+    for n in range(PLACE_PIECES):
+        r = pl.ds(n * part, part)
+        loads.append(pltpu.make_async_copy(x.at[r], xt.at[r], sem_in.at[n]))
+        stores.append(pltpu.make_async_copy(xt.at[r], xo.at[r], sem_out.at[n]))
+    for n, (src, mid, dst) in enumerate(((kn, kt, ko), (vn, vt, vo))):
+        loads.append(pltpu.make_async_copy(src, mid, sem_in.at[PLACE_PIECES + n]))
+        stores.append(pltpu.make_async_copy(mid, dst, sem_out.at[PLACE_PIECES + n]))
+    for c in loads:
+        c.start()
+    for a, b in zip(loads, stores):
+        a.wait()
+        b.start()
+    for c in stores:
+        c.wait()
 
 
 def solution(mesh):
@@ -475,6 +510,15 @@
                 collective_id=0, has_side_effects=True, vmem_limit_bytes=67043328),
         )(x_in, w_q, w_k, w_v, w_o, w_gate, w_up, w_down, norm_gain, k_cache, v_cache,
           lengths.reshape(1, rows), freq)
+        results = (x_out, k_new, v_new)
+        x_out, k_new, v_new = pl.pallas_call(
+            place,
+            out_shape=tuple(jax.ShapeDtypeStruct(a.shape, a.dtype) for a in results),
+            in_specs=[hbm] * 3,
+            out_specs=(hbm,) * 3,
+            scratch_shapes=[pltpu.VMEM(a.shape, a.dtype) for a in results]
+            + [dma((PLACE_PIECES + 2,)), dma((PLACE_PIECES + 2,))],
+        )(*results)
         return x_out, k_new.reshape(layers, rows, 1, head), v_new.reshape(layers, rows, 1, head)
 
     return jax.shard_map(per_device, mesh=mesh, in_specs=arg_specs, out_specs=(row_spec, new_spec, new_spec),

time: 108 us -> 90.2 us (0.84)
  Pallas kernels: 101 us -> 89.3 us
  local copies, waits for them, and re-layouts: 6.26 us -> 0 us
    pallas_call x1, Pallas kernels: 101 us -> 86.8 us  [per_device(): pl.pallas_call(functools.partial(kernel, dims), out_shape=(jax.ShapeDtype...]
    unnamed x3 -> x0, local copies, waits for them, and re-layouts: 6.26 us -> none
    pallas_call x0 -> x1, Pallas kernels: none -> 2.51 us  [per_device(): pl.pallas_call(place, out_shape=tuple((jax.ShapeDtypeStruct(a.shape, a.dt...]
where the time goes in v1:
time: 90.2 us; the launch traced here: 90 us
  Pallas kernels  89.3 us (99%)
    pallas_call x1, Pallas kernels, per_device(): pl.pallas_call(functools.partial(kernel, dims), out_shape=(jax.ShapeDtype...  86.8 us
    pallas_call x1, Pallas kernels, per_device(): pl.pallas_call(place, out_shape=tuple((jax.ShapeDtypeStruct(a.shape, a.dt...  2.51 us

profile of v1, /device:TPU:113, one launch (start us, length us, event | category | flops | bytes accessed | tf_op | source)
XLA Modules:
  0.0 90.0 jit_solution(1401102949808561671)
XLA Ops:
  0.6 86.8 %shard_map.148 = (bf16[256,4096]{1,0:T(8,128)(2,1)}, bf16[2,256,128]{2,1,0:T(8,128)(2,1)}, bf16[2,256,128]{2,1,0:T(8,128)(2,1)}) custom-call(bf16[256,4096]{1,0:T(8,128)(2,1)} %x_hbm.1, bf16[2,4096,512]{2,1,0:T(8,128)(2,1)} %wq.1, bf16[2,4096,128]{2,1,0:T(8,128)(2,1)} %wk.1, bf16[2,4096,128]{2,1,0:T(8,128)(2,1)} %wv.1, bf16[2,512,4096]{2,1,0:T(8,128)(2,1)} %wo.1, ...), custom_call_target="tpu_custom_call" | custom-call | tf_op jit(solution)/shard_map/pallas_call | solution.py:463
  87.5 2.5 %shard_map.149 = (bf16[256,4096]{1,0:T(8,128)(2,1)}, bf16[2,256,128]{2,1,0:T(8,128)(2,1)}, bf16[2,256,128]{2,1,0:T(8,128)(2,1)}) custom-call(bf16[256,4096]{1,0:T(8,128)(2,1)} %get-tuple-element.9.x, bf16[2,256,128]{2,1,0:T(8,128)(2,1)} %get-tuple-element.10.kn, bf16[2,256,128]{2,1,0:T(8,128)(2,1)} %get-tuple-element.11.vn), custom_call_target="tpu_custom_call" | custom-call | tf_op jit(solution)/shard_map/pallas_call | solution.py:514

commit v2 on v1

--- a/solution.py
+++ b/solution.py
@@ -22,11 +22,11 @@
 GROUPS = 4
 
 
-def kernel(dims, x_hbm, wq, wk, wv, wo, wg, wu, wd, gain, kc, vc, lens, freq,
+def kernel(dims, x_hbm, wq, wk, wv, wo, wg, wu, wd, gain_hbm, kc, vc, lens_hbm, freq_hbm,
            xo, kn, vn,
            xb, acc, hb, wa, wb, kb, vb, lhs, qs, ks, vs, ob, lenb, cosb, sinb, rowscale, gains, kst, vst,
-           send_d, recv_d, send_o, send_r, send_l, opp_t, opp_b, from_l, from_r, own, hold_r, hold_l, stat_s, stat_r,
-           sem_a, sem_kv, sem_b, sem_x, sem_kn,
+           gain, lens, freq, send_d, recv_d, send_o, send_r, send_l, opp_t, opp_b, from_l, from_r, own, hold_r, hold_l, stat_s, stat_r,
+           sem_a, sem_kv, sem_b, sem_x, sem_kn, sem_s,
            d_send, d_recv, o_send, o_recv, r_send, l_send, fl_recv, fr_recv,
            ag_send, ag_fwd, ag_ring, ag_recv, st_send, st_recv):
     layers, rows, width, q_width, head, ff, cache_len, members = dims
@@ -55,15 +55,34 @@
         turn = (g + (g // 2) * (2 * g - 3)) % 4
         if q % 2:
             turn = (4 - turn) % 4
-        c = core if q < 2 else 1 - core
+        c = (core + q // 2) % 2
         return 2 * (2 * ((chip + turn) % chips) + c) + q % 2
+
+    def step_chunk(i, ab):
+        g = i // 2
+        turn = (g + (g // 2) * (2 * g - 3)) % 4
+        if ab:
+            turn = (4 - turn) % 4
+        return 2 * (2 * ((chip + turn) % chips) + (core + i) % 2) + ab
+
+    def step_copies(l, i, which=range(2)):
+        out = []
+        for ab in which:
+            row = pl.multiple_of(step_chunk(i, ab) * chunk, chunk)
+            at = pl.multiple_of((i % 2) * 2 * chunk, chunk) + ab * chunk
+            for n, (w, to, size) in enumerate(cols):
+                out.append(pltpu.make_async_copy(
+                    w.at[l, pl.ds(row, chunk), :],
+                    wa.at[(i // 2) % 2, pl.ds(at, chunk), pl.ds(to, size)],
+                    sem_a.at[(i // 2) % 2, (i % 2) * 2 + ab, n]))
+        return out
 
     cols = ((wq, 0, q_width), (wk, q_width, head), (wv, q_width + head, head),
             (wg, q_width + 2 * head, ff), (wu, q_width + 2 * head + ff, ff))
 
-    def a_copies(l, g, slot, which=range(5)):
+    def a_copies(l, g, slot, which=range(5), parts=range(4)):
         out = []
-        for q in range(4):
+        for q in parts:
             row = pl.multiple_of(chunk_id(g, q) * chunk, chunk)
             for n in which:
                 w, at, size = cols[n]
@@ -75,22 +94,34 @@
 
     piece = rows // KV_PIECES
 
-    def start_kv(l):
+    def start_kv(l, n):
         for p in range(KV_PIECES):
-            start(kv_copies(l, p))
+            kv_copy(l, p, n).start()
+
+    def kv_copy(l, p, n):
+        src, dst = ((kc, kb), (vc, vb))[n]
+        at = pl.ds(p * piece, piece)
+        return pltpu.make_async_copy(src.at[l, at, 0], dst.at[at], sem_kv.at[n, p])
+
+    def start_kv(l, n):
+        for p in range(KV_PIECES):
+            kv_copy(l, p, n).start()
 
     def kv_copies(l, p):
         at = pl.multiple_of(p * piece, piece)
         return [pltpu.make_async_copy(src.at[l, pl.ds(at, piece), 0], dst.at[pl.ds(at, piece)], sem_kv.at[n, p])
                 for n, (src, dst) in enumerate(((kc, kb), (vc, vb)))]
 
-    def b_copies(l):
-        out = [pltpu.make_async_copy(wo.at[l], wb.at[pl.ds(0, q_width)], sem_b.at[0])]
-        part = ff // 4
+    b_order = (opp_chip, right_chip, left_chip, chip)
+
+    def b_copies(l, n):
+        at = pl.ds(pl.multiple_of(b_order[n] * 2 * blk, 2 * blk), 2 * blk)
+        return [pltpu.make_async_copy(wo.at[l, :, at], wb.at[pl.ds(0, q_width), at], sem_b.at[n, 0]),
+                pltpu.make_async_copy(wd.at[l, :, at], wb.at[pl.ds(q_width, ff), at], sem_b.at[n, 1])]
+
+    def start_b(l):
         for n in range(4):
-            out.append(pltpu.make_async_copy(
-                wd.at[l, pl.ds(n * part, part), :], wb.at[pl.ds(q_width + n * part, part)], sem_b.at[1 + n]))
-        return out
+            start(b_copies(l, n))
 
     def x_copy(n):
         return pltpu.make_async_copy(x_hbm.at[:, pl.ds(n * chunk, chunk)], xb.at[n], sem_x.at[n])
@@ -118,6 +149,8 @@
         return remote(send_d.at[n], recv_d.at[n], d_send.at[n], d_recv.at[n], mate)
 
     top, bottom = pl.ds(0, half), pl.ds(half, half)
+    mate_top = remote(send_d.at[0, top], recv_d.at[0, top], d_send.at[0], d_recv.at[0], mate)
+    mate_bottom = remote(send_d.at[0, bottom], recv_d.at[0, bottom], d_send.at[4], d_recv.at[4], mate)
     opp_right = remote(send_o.at[top], opp_t, o_send.at[0], o_recv.at[0], right)
     opp_left = remote(send_o.at[bottom], opp_b, o_send.at[1], o_recv.at[1], left)
     right_top = remote(send_r.at[top], from_l.at[top], r_send.at[0], fl_recv.at[0], right)
@@ -160,9 +193,9 @@
             arrived(chunk_id(g, q))
 
     def sum_drain():
-        for n in range(4):
+        for n in range(1, 4):
             mate_copy(n).wait_send()
-        for c in (opp_right, opp_left, right_top, right_bottom, left_top, left_bottom):
+        for c in (mate_top, mate_bottom, opp_right, opp_left, right_top, right_bottom, left_top, left_bottom):
             c.wait_send()
 
     def gather_drain():
@@ -178,14 +211,17 @@
         to = (me + k) % members
         return remote(stat_s, stat_r.at[k - 1], st_send.at[k - 1], st_recv.at[k - 1], to)
 
+    small = [pltpu.make_async_copy(a, b, sem_s.at[n])
+             for n, (a, b) in enumerate(((lens_hbm, lens), (freq_hbm, freq), (gain_hbm, gain)))]
+    start(small)
     for n in range(width // chunk):
         x_copy(n).start()
-    start(a_copies(0, 0, 0))
+    start(step_copies(0, 0, (0,)))
     barrier = pltpu.get_barrier_semaphore()
     for k in range(1, members):
         pl.semaphore_signal(barrier, inc=1, device_id=dev((me + k) % members), device_id_type=MESH)
-    start(a_copies(0, 1, 1))
-
+    wait(small)
+    start(step_copies(0, 0, (1,)))
     len_f = jnp.transpose(jnp.broadcast_to(lens[...].astype(F32), (head, rows)))
     lenb[...] = len_f
     angle = len_f * freq[...]
@@ -193,22 +229,22 @@
     lane = lax.broadcasted_iota(jnp.int32, (rows, head), 1)
     sin = jnp.sin(angle)
     sinb[...] = jnp.where(lane < head // 2, -sin, sin)
+    for n in range(width // chunk):
+        x_copy(n).wait()
+    start(step_copies(0, 1))
     g32 = gain[...].astype(F32)
     for l in range(layers):
         gains[l] = g32[l:l + 1]
-
     total = jnp.zeros((rows, chunk), F32)
     for n in range(width // chunk):
-        x_copy(n).wait()
         v = xb[n].astype(F32)
         total = total + v * v
     mean = jnp.sum(total, axis=1, keepdims=True) / width
     rowscale[...] = jnp.broadcast_to(lax.rsqrt(mean + NORM_EPS), (rows, head))
-    pl.semaphore_wait(barrier, members - 1)
 
     scale = 1.0 / math.sqrt(head)
 
-    def layer(l, _):
+    def layer(l):
         def norm_from_stats():
             s = stat_s[...]
             for k in range(1, members):
@@ -219,35 +255,82 @@
             rowscale[...] = jnp.transpose(jnp.broadcast_to(r, (head, rows)))
         when(l > 0, norm_from_stats)
 
-        def group(g, _):
-            slot = g % 2
-            when(l > 0, lambda: gather_mate(g))
+        def normed_chunk(n):
             r = rowscale[...]
             r = jnp.concatenate([r] * (chunk // head), axis=1)
-            for q in range(4):
-                n = chunk_id(g, q)
-                gv = gains[l, :, pl.ds(pl.multiple_of(n * chunk, chunk), chunk)]
-                hb[:, q * chunk:(q + 1) * chunk] = (xb[n].astype(F32) * r * gv).astype(BF16)
-            wait(a_copies(l, g, slot))
-
-            def product(at, end):
-                d = jnp.dot(hb[...], wa[slot, :, at:end], preferred_element_type=F32)
-                acc[:, at:end] = jnp.where(g == 0, d, acc[:, at:end] + d)
-
-            cuts = list(range(0, n_in, 512)) + [n_in]
-            gate_end = q_width + 2 * head + ff
-            middle = next(n for n, at in enumerate(cuts) if at >= gate_end)
-            for at, end in zip(cuts[:middle], cuts[1:middle + 1]):
-                product(at, end)
-            when(g < GROUPS - 2, lambda: start(a_copies(l, g + 2, slot, range(4))))
-            pl.when(jnp.logical_and(l > 0, g < GROUPS - 1))(lambda: gather_links(g + 1))
-            pl.when(jnp.logical_and(l == 0, g == GROUPS - 2))(lambda: start_kv(l))
-            for at, end in zip(cuts[middle:-1], cuts[middle + 1:]):
-                product(at, end)
-            when(g < GROUPS - 2, lambda: start(a_copies(l, g + 2, slot, range(4, 5))))
-            pl.when(jnp.logical_and(l == 0, g == GROUPS - 2))(lambda: start(b_copies(l)))
-            return 0
-        lax.fori_loop(0, GROUPS, group, 0)
+            gv = gains[l, :, pl.ds(pl.multiple_of(n * chunk, chunk), chunk)]
+            return (xb[n].astype(F32) * r * gv).astype(BF16)
+
+        def normed(g, qs):
+            for q in qs:
+                hb[:, (4 * g + q) * chunk:(4 * g + q + 1) * chunk] = normed_chunk(chunk_id(g, q))
+
+        cuts = list(range(0, n_in, 512)) + [n_in]
+        gate_end = q_width + 2 * head + ff
+        middle = next(n for n, at in enumerate(cuts) if at >= gate_end)
+
+        def products(g, spans):
+            for at, end in spans:
+                d = jnp.dot(hb[:, 4 * g * chunk:4 * (g + 1) * chunk], wa[g % 2, :, at:end], preferred_element_type=F32)
+                acc[:, at:end] = d if g == 0 else acc[:, at:end] + d
+
+        spans = list(zip(cuts[:-1], cuts[1:]))
+
+        def stream_step(i, first):
+            wait(step_copies(l, i))
+            k_at = pl.ds(pl.multiple_of(i * 2 * chunk, 2 * chunk), 2 * chunk)
+            rows_at = pl.ds(pl.multiple_of((i % 2) * 2 * chunk, chunk), 2 * chunk)
+            for at, end in spans:
+                d = jnp.dot(hb[:, k_at], wa[(i // 2) % 2, rows_at, at:end], preferred_element_type=F32)
+                acc[:, at:end] = d if first else acc[:, at:end] + d
+
+        if l == 0:
+            for g in range(GROUPS):
+                normed(g, range(4))
+            start(step_copies(l, 2))
+            start(step_copies(l, 3))
+            stream_step(0, True)
+            start(step_copies(l, 4))
+
+            def stream(i, _):
+                stream_step(i, False)
+                start(step_copies(l, i + 4))
+                return 0
+            lax.fori_loop(1, 4, stream, 0)
+
+            def group(g, _):
+                slot = g % 2
+                wait(a_copies(l, g, slot))
+                k_at = pl.ds(pl.multiple_of(g * 4 * chunk, 4 * chunk), 4 * chunk)
+                for at, end in spans:
+                    acc[:, at:end] += jnp.dot(hb[:, k_at], wa[slot, :, at:end], preferred_element_type=F32)
+
+                def after_two():
+                    start_kv(l, 0)
+                    start_kv(l, 1)
+                pl.when(g == 2)(after_two)
+
+                def after_three():
+                    start(b_copies(l, 0))
+                    start(b_copies(l, 1))
+                pl.when(g == 3)(after_three)
+                return 0
+            lax.fori_loop(2, GROUPS, group, 0)
+        else:
+            for g in range(GROUPS):
+                slot = g % 2
+                gather_mate(g)
+                normed(g, range(4) if g == 0 else range(2, 4))
+                wait(a_copies(l, g, slot))
+                products(g, spans[:middle])
+                if g < GROUPS - 2:
+                    start(a_copies(l, g + 2, slot, range(4)))
+                if g < GROUPS - 1:
+                    gather_links(g + 1)
+                    normed(g + 1, range(2))
+                products(g, spans[middle:])
+                if g < GROUPS - 2:
+                    start(a_copies(l, g + 2, slot, range(4, 5)))
 
         cosv, sinv = cosb[...], sinb[...]
         for h in range(heads):
@@ -268,6 +351,9 @@
             uv = acc[:, gate_at + ff + at:gate_at + ff + at + 256]
             lhs[:, q_width + at:q_width + at + 256] = (gv * jax.nn.sigmoid(gv) * uv).astype(BF16)
 
+        if l == 0:
+            start(b_copies(l, 2))
+            start(b_copies(l, 3))
         tiles = ROW_GROUP * cache_len // head
         per_tile = head // cache_len
         r_id = lax.broadcasted_iota(jnp.int32, (1, ROW_GROUP, head), 1)
@@ -303,7 +389,7 @@
                 ob[at:at + ROW_GROUP, h * head:(h + 1) * head] = o[h]
 
         for p in range(KV_PIECES):
-            wait(kv_copies(l, p))
+            wait(kv_copy(l, p, n) for n in range(2))
         step = STEP_ROWS
         groups_at = [list(range(b, b + step, ROW_GROUP)) for b in range(0, rows, step)]
         picks, wts = {}, {}
@@ -319,11 +405,6 @@
                     wts[at] = weights(at, picks.pop(at))
         lhs[:, 0:q_width] = ob[...].astype(BF16)
 
-        def prefetch():
-            start(a_copies(l + 1, 0, 0))
-            start_kv(l + 1)
-            start(a_copies(l + 1, 1, 1))
-        when(l < layers - 1, prefetch)
         wait(kn_copies(l))
 
         def drain():
@@ -333,44 +414,53 @@
                 stat_copy(k).wait_send()
         when(l > 0, drain)
 
-        wait(b_copies(l))
+        wait(b_copies(l, 0))
+        if l == 0:
+            pl.semaphore_wait(barrier, members - 1)
 
         def share(i):
             at = pl.multiple_of(i * blk, blk)
             return jnp.dot(lhs[...], wb[:, pl.ds(at, blk)], preferred_element_type=F32)
 
         send_d[0] = share(2 * opp_chip + 1 - core).astype(BF16)
-        mate_copy(0).start()
+        mate_top.start()
+        mate_bottom.start()
         own[...] = share(2 * opp_chip + core)
+        mate_top.wait_recv()
+        send_o[top] = (own[top] + recv_d[0, top].astype(F32)).astype(BF16)
+        opp_right.start()
+        mate_bottom.wait_recv()
+        send_o[bottom] = (own[bottom] + recv_d[0, bottom].astype(F32)).astype(BF16)
+        opp_left.start()
+        wait(b_copies(l, 1))
+        wait(b_copies(l, 2))
         send_d[1] = share(2 * right_chip + 1 - core).astype(BF16)
+        send_d[2] = share(2 * left_chip + 1 - core).astype(BF16)
         mate_copy(1).start()
-        mate_copy(0).wait_recv()
-        send_o[...] = (own[...] + recv_d[0].astype(F32)).astype(BF16)
-        opp_right.start()
-        opp_left.start()
-        send_d[2] = share(2 * left_chip + 1 - core).astype(BF16)
         mate_copy(2).start()
-        t = share(right)
+        hold_r[...] = share(right)
+        hold_l[...] = share(left)
         mate_copy(1).wait_recv()
-        t = t + recv_d[1].astype(F32)
-        send_r[bottom] = t[half:].astype(BF16)
+        send_r[bottom] = (hold_r[bottom] + recv_d[1, bottom].astype(F32)).astype(BF16)
         right_bottom.start()
-        hold_r[...] = t[:half]
-        t = share(left)
         mate_copy(2).wait_recv()
-        t = t + recv_d[2].astype(F32)
-        send_l[top] = t[:half].astype(BF16)
+        send_l[top] = (hold_l[top] + recv_d[2, top].astype(F32)).astype(BF16)
         left_top.start()
-        hold_l[...] = t[half:]
+        wait(b_copies(l, 3))
+        if l < layers - 1:
+            start(a_copies(l + 1, 0, 0))
+            start(a_copies(l + 1, 1, 1))
+            start_kv(l + 1, 0)
+            start_kv(l + 1, 1)
         send_d[3] = share(mate).astype(BF16)
+        own[...] = share(me)
         mate_copy(3).start()
-        own[...] = share(me)
-        when(l < layers - 1, lambda: start(b_copies(l + 1)))
+        when(l < layers - 1, lambda: start_b(l + 1))
         opp_right.wait_recv()
-        send_r[top] = (hold_r[...] + opp_t[...].astype(F32)).astype(BF16)
+        send_r[top] = (hold_r[top] + recv_d[1, top].astype(F32) + opp_t[...].astype(F32)).astype(BF16)
         right_top.start()
         opp_left.wait_recv()
-        send_l[bottom] = (hold_l[...] + opp_b[...].astype(F32)).astype(BF16)
+        send_l[bottom] = (hold_l[bottom] + recv_d[2, bottom].astype(F32) + opp_b[...].astype(F32)).astype(BF16)
         left_bottom.start()
         mate_copy(3).wait_recv()
         x_old = jnp.concatenate([xb[own_a], xb[own_b]], axis=1).astype(F32)
@@ -396,9 +486,9 @@
         when(l < layers - 1, send_stats)
         for c in own_sends:
             c.start()
-        return 0
-
-    lax.fori_loop(0, layers, layer, 0)
+
+    for l in range(layers):
+        layer(l)
 
     out_copy(own_a).start()
     out_copy(own_b).start()
@@ -457,7 +547,6 @@
         n_in = q_width + 2 * head + 2 * ff
         inv = np.float32(ROPE_BASE) ** (-np.arange(head // 2, dtype=np.float32) / np.float32(head // 2))
         freq = jnp.asarray(np.concatenate([inv, inv])[None].astype(np.float32))
-        vmem = pl.BlockSpec(memory_space=pltpu.VMEM)
         hbm = pl.BlockSpec(memory_space=pl.ANY)
         dma = pltpu.SemaphoreType.DMA
         x_out, k_new, v_new = pl.pallas_call(
@@ -465,12 +554,12 @@
             out_shape=(jax.ShapeDtypeStruct((rows, width), BF16),
                        jax.ShapeDtypeStruct((layers, rows, head), BF16),
                        jax.ShapeDtypeStruct((layers, rows, head), BF16)),
-            in_specs=[hbm] * 8 + [vmem, hbm, hbm, vmem, vmem],
+            in_specs=[hbm] * 13,
             out_specs=(hbm, hbm, hbm),
             scratch_shapes=[
                 pltpu.VMEM((width // chunk, rows, chunk), BF16),
                 pltpu.VMEM((rows, n_in), F32),
-                pltpu.VMEM((rows, 4 * chunk), BF16),
+                pltpu.VMEM((rows, width), BF16),
                 pltpu.VMEM((2, 4 * chunk, n_in), BF16),
                 pltpu.VMEM((q_width + ff, width), BF16),
                 pltpu.VMEM((rows, cache_len, head), BF16),
@@ -487,6 +576,9 @@
                 pltpu.VMEM((layers, 1, width), F32),
                 pltpu.VMEM((rows, head), BF16),
                 pltpu.VMEM((rows, head), BF16),
+                pltpu.VMEM((layers, width), BF16),
+                pltpu.VMEM((1, rows), jnp.int32),
+                pltpu.VMEM((1, head), F32),
                 pltpu.VMEM((4, rows, blk), BF16),
                 pltpu.VMEM((4, rows, blk), BF16),
                 pltpu.VMEM((rows, blk), BF16),
@@ -497,12 +589,12 @@
                 pltpu.VMEM((rows, blk), BF16),
                 pltpu.VMEM((rows, blk), BF16),
                 pltpu.VMEM((rows, blk), F32),
-                pltpu.VMEM((half, blk), F32),
-                pltpu.VMEM((half, blk), F32),
+                pltpu.VMEM((rows, blk), F32),
+                pltpu.VMEM((rows, blk), F32),
                 pltpu.VMEM((8, rows), F32),
                 pltpu.VMEM((members - 1, 8, rows), F32),
-                dma((2, 4, 5)), dma((2, KV_PIECES)), dma((5,)), dma((width // chunk,)), dma((2,)),
-                dma((4,)), dma((4,)), dma((2,)), dma((2,)), dma((2,)), dma((2,)), dma((2,)), dma((2,)),
+                dma((2, 4, 5)), dma((2, KV_PIECES)), dma((4, 2)), dma((width // chunk,)), dma((2,)), dma((3,)),
+                dma((5,)), dma((5,)), dma((2,)), dma((2,)), dma((2,)), dma((2,)), dma((2,)), dma((2,)),
                 dma((6,)), dma((GROUPS, 2)), dma((2,)), dma((width // chunk,)),
                 dma((members - 1,)), dma((members - 1,)),
             ],

time: 90.2 us -> 84.7 us (0.939)
  Pallas kernels: 89.3 us -> 83.7 us
    pallas_call x1, Pallas kernels: 86.8 us -> 81.2 us  [per_device(): pl.pallas_call(functools.partial(kernel, dims), out_shape=(jax.ShapeDtype...]
where the time goes in v2:
time: 84.7 us; the launch traced here: 84.5 us
  Pallas kernels  83.7 us (99%)
    pallas_call x1, Pallas kernels, per_device(): pl.pallas_call(functools.partial(kernel, dims), out_shape=(jax.ShapeDtype...  81.2 us
    pallas_call x1, Pallas kernels, per_device(): pl.pallas_call(place, out_shape=tuple((jax.ShapeDtypeStruct(a.shape, a.dt...  2.51 us

profile of v2, /device:TPU:113, one launch (start us, length us, event | category | flops | bytes accessed | tf_op | source)
XLA Modules:
  0.0 84.5 jit_solution(4404256976454328289)
XLA Ops:
  0.6 81.2 %shard_map.148 = (bf16[256,4096]{1,0:T(8,128)(2,1)}, bf16[2,256,128]{2,1,0:T(8,128)(2,1)}, bf16[2,256,128]{2,1,0:T(8,128)(2,1)}) custom-call(bf16[256,4096]{1,0:T(8,128)(2,1)} %x_hbm.1, bf16[2,4096,512]{2,1,0:T(8,128)(2,1)} %wq.1, bf16[2,4096,128]{2,1,0:T(8,128)(2,1)} %wk.1, bf16[2,4096,128]{2,1,0:T(8,128)(2,1)} %wv.1, bf16[2,512,4096]{2,1,0:T(8,128)(2,1)} %wo.1, ...), custom_call_target="tpu_custom_call" | custom-call | tf_op jit(solution)/shard_map/pallas_call | solution.py:552
  81.8 2.5 %shard_map.149 = (bf16[256,4096]{1,0:T(8,128)(2,1)}, bf16[2,256,128]{2,1,0:T(8,128)(2,1)}, bf16[2,256,128]{2,1,0:T(8,128)(2,1)}) custom-call(bf16[256,4096]{1,0:T(8,128)(2,1)} %get-tuple-element.9.x, bf16[2,256,128]{2,1,0:T(8,128)(2,1)} %get-tuple-element.10.kn, bf16[2,256,128]{2,1,0:T(8,128)(2,1)} %get-tuple-element.11.vn), custom_call_target="tpu_custom_call" | custom-call | tf_op jit(solution)/shard_map/pallas_call | solution.py:606

commit v3 on v2

--- a/solution.py
+++ b/solution.py
@@ -19,6 +19,7 @@
 STEP_ROWS = 32
 KV_PIECES = 4
 PLACE_PIECES = 8
+PHASES = ((0, 1), (2,), (3, 4), (5, 6), (7,))
 GROUPS = 4
 
 
@@ -216,12 +217,12 @@
     start(small)
     for n in range(width // chunk):
         x_copy(n).start()
-    start(step_copies(0, 0, (0,)))
+    start(step_copies(0, 0))
     barrier = pltpu.get_barrier_semaphore()
     for k in range(1, members):
         pl.semaphore_signal(barrier, inc=1, device_id=dev((me + k) % members), device_id_type=MESH)
     wait(small)
-    start(step_copies(0, 0, (1,)))
+    start(step_copies(0, 1))
     len_f = jnp.transpose(jnp.broadcast_to(lens[...].astype(F32), (head, rows)))
     lenb[...] = len_f
     angle = len_f * freq[...]
@@ -231,7 +232,7 @@
     sinb[...] = jnp.where(lane < head // 2, -sin, sin)
     for n in range(width // chunk):
         x_copy(n).wait()
-    start(step_copies(0, 1))
+    start(step_copies(0, 2))
     g32 = gain[...].astype(F32)
     for l in range(layers):
         gains[l] = g32[l:l + 1]
@@ -266,30 +267,26 @@
                 hb[:, (4 * g + q) * chunk:(4 * g + q + 1) * chunk] = normed_chunk(chunk_id(g, q))
 
         cuts = list(range(0, n_in, 512)) + [n_in]
-        gate_end = q_width + 2 * head + ff
-        middle = next(n for n, at in enumerate(cuts) if at >= gate_end)
-
-        def products(g, spans):
-            for at, end in spans:
-                d = jnp.dot(hb[:, 4 * g * chunk:4 * (g + 1) * chunk], wa[g % 2, :, at:end], preferred_element_type=F32)
-                acc[:, at:end] = d if g == 0 else acc[:, at:end] + d
-
         spans = list(zip(cuts[:-1], cuts[1:]))
 
-        def stream_step(i, first):
+        def stream_step(i, first, beside=lambda: None):
             wait(step_copies(l, i))
+            beside()
             k_at = pl.ds(pl.multiple_of(i * 2 * chunk, 2 * chunk), 2 * chunk)
             rows_at = pl.ds(pl.multiple_of((i % 2) * 2 * chunk, chunk), 2 * chunk)
             for at, end in spans:
                 d = jnp.dot(hb[:, k_at], wa[(i // 2) % 2, rows_at, at:end], preferred_element_type=F32)
                 acc[:, at:end] = d if first else acc[:, at:end] + d
 
+        def rest():
+            normed(0, range(2, 4))
+            for g in range(1, GROUPS):
+                normed(g, range(4))
+
         if l == 0:
-            for g in range(GROUPS):
-                normed(g, range(4))
-            start(step_copies(l, 2))
+            normed(0, range(2))
             start(step_copies(l, 3))
-            stream_step(0, True)
+            stream_step(0, True, rest)
             start(step_copies(l, 4))
 
             def stream(i, _):
@@ -317,20 +314,26 @@
                 return 0
             lax.fori_loop(2, GROUPS, group, 0)
         else:
-            for g in range(GROUPS):
-                slot = g % 2
-                gather_mate(g)
-                normed(g, range(4) if g == 0 else range(2, 4))
-                wait(a_copies(l, g, slot))
-                products(g, spans[:middle])
-                if g < GROUPS - 2:
-                    start(a_copies(l, g + 2, slot, range(4)))
-                if g < GROUPS - 1:
-                    gather_links(g + 1)
-                    normed(g + 1, range(2))
-                products(g, spans[middle:])
-                if g < GROUPS - 2:
-                    start(a_copies(l, g + 2, slot, range(4, 5)))
+            gather_mate(0)
+            normed(0, range(4))
+            for n, steps in enumerate(PHASES):
+                for i in steps:
+                    wait(step_copies(l, i))
+                for at, end in spans:
+                    d = sum(jnp.dot(hb[:, i * 2 * chunk:(i + 1) * 2 * chunk],
+                                    wa[i // 2 % 2, i % 2 * 2 * chunk:(i % 2 + 1) * 2 * chunk, at:end],
+                                    preferred_element_type=F32) for i in steps)
+                    acc[:, at:end] = d if n == 0 else acc[:, at:end] + d
+                for i in steps:
+                    if i + 4 < 2 * GROUPS:
+                        start(step_copies(l, i + 4))
+                if n + 1 < GROUPS:
+                    gather_links(n + 1)
+                if n > 0 and n < GROUPS:
+                    gather_mate(n)
+                    normed(n, range(2, 4))
+                if n + 1 < GROUPS:
+                    normed(n + 1, range(2))
 
         cosv, sinv = cosb[...], sinb[...]
         for h in range(heads):
@@ -448,8 +451,8 @@
         left_top.start()
         wait(b_copies(l, 3))
         if l < layers - 1:
-            start(a_copies(l + 1, 0, 0))
-            start(a_copies(l + 1, 1, 1))
+            for i in range(4):
+                start(step_copies(l + 1, i))
             start_kv(l + 1, 0)
             start_kv(l + 1, 1)
         send_d[3] = share(mate).astype(BF16)

time: 84.7 us -> 83.7 us (0.988)
  Pallas kernels: 83.7 us -> 82.8 us
    pallas_call x1, Pallas kernels: 81.2 us -> 80.3 us  [per_device(): pl.pallas_call(functools.partial(kernel, dims), out_shape=(jax.ShapeDtype...]
where the time goes in v3:
time: 83.7 us; the launch traced here: 83.6 us
  Pallas kernels  82.8 us (99%)
    pallas_call x1, Pallas kernels, per_device(): pl.pallas_call(functools.partial(kernel, dims), out_shape=(jax.ShapeDtype...  80.3 us
    pallas_call x1, Pallas kernels, per_device(): pl.pallas_call(place, out_shape=tuple((jax.ShapeDtypeStruct(a.shape, a.dt...  2.51 us

profile of v3, /device:TPU:113, one launch (start us, length us, event | category | flops | bytes accessed | tf_op | source)
XLA Modules:
  0.0 83.6 jit_solution(7715621160788376675)
XLA Ops:
  0.6 80.3 %shard_map.148 = (bf16[256,4096]{1,0:T(8,128)(2,1)}, bf16[2,256,128]{2,1,0:T(8,128)(2,1)}, bf16[2,256,128]{2,1,0:T(8,128)(2,1)}) custom-call(bf16[256,4096]{1,0:T(8,128)(2,1)} %x_hbm.1, bf16[2,4096,512]{2,1,0:T(8,128)(2,1)} %wq.1, bf16[2,4096,128]{2,1,0:T(8,128)(2,1)} %wk.1, bf16[2,4096,128]{2,1,0:T(8,128)(2,1)} %wv.1, bf16[2,512,4096]{2,1,0:T(8,128)(2,1)} %wo.1, ...), custom_call_target="tpu_custom_call" | custom-call | tf_op jit(solution)/shard_map/pallas_call | solution.py:555
  80.9 2.5 %shard_map.149 = (bf16[256,4096]{1,0:T(8,128)(2,1)}, bf16[2,256,128]{2,1,0:T(8,128)(2,1)}, bf16[2,256,128]{2,1,0:T(8,128)(2,1)}) custom-call(bf16[256,4096]{1,0:T(8,128)(2,1)} %get-tuple-element.9.x, bf16[2,256,128]{2,1,0:T(8,128)(2,1)} %get-tuple-element.10.kn, bf16[2,256,128]{2,1,0:T(8,128)(2,1)} %get-tuple-element.11.vn), custom_call_target="tpu_custom_call" | custom-call | tf_op jit(solution)/shard_map/pallas_call | solution.py:609
